TPU v7x, 32 devices: a whole 2x2x4 slice. The times are simulated.
32 devices in a mesh: rep: 16 (over z, y, core), tp: 2 (over x).
Axes of the slice: x: 2, y: 2, z: 4, core: 2. Of those that a mesh axis runs over, the one named last changes fastest.
Arguments:
- activations: bfloat16 [8192, 6144], P('rep', 'tp'), may hold values from -6 to 6
- norm_gain: float32 [6144], replicated, may hold values from 0.5 to 1.5
- query_gain: float32 [128], replicated, may hold values from 0.5 to 18
- key_gain: float32 [128], replicated, may hold values from 0.5 to 18
- project_in: bfloat16 [6144, 24, 384], P('rep', 'tp'), may hold values from -1 to 1
- project_out: bfloat16 [6144, 3072], P('rep', 'tp'), may hold values from -1 to 1
Outputs:
- attended: bfloat16 [8192, 6144], P('rep', 'tp')
- weight_norms: float32 [2], replicated
All inputs are finite; a program needn't handle non-finite values.
Results may differ from a plain program's by a relative error of at most 0.018.
The roundings to bfloat16 on the way count: a program that leaves them out, or rounds other values in their place, can miss the bound.
Values may be sent and summed in bfloat16 or wider, within the bound.
A program may use at most 192 MiB of HBM per device.

v0:
```python
import math
import jax
import jax.numpy as jnp
from jax import lax
from jax.sharding import PartitionSpec as P

D = 6144
HEADS = 24
HEAD_DIM = 128
PATCHES = 256


def layer_norm(values, gain):
    average = jnp.mean(values, -1, keepdims=True)
    centred = values - average
    variance = jnp.mean(centred * centred, -1, keepdims=True)
    return centred * lax.rsqrt(variance + 1e-06) * gain


def shards(activations, norm_gain, query_gain, key_gain, project_in, project_out):
    gathered_rows = lax.all_gather(activations, "tp", axis=1, tiled=True)
    normed = layer_norm(gathered_rows.astype(jnp.float32), norm_gain).astype(jnp.bfloat16)
    tok_rows = normed.shape[0]
    local_heads = project_in.shape[1]
    head_dim = project_in.shape[2] // 3
    piece = lax.all_gather(project_in, "rep", axis=0, tiled=True)
    running = jnp.dot(normed, piece.reshape(piece.shape[0], -1), preferred_element_type=jnp.float32)
    projected = running
    images_here = tok_rows // PATCHES
    projected = projected.reshape(images_here, PATCHES, local_heads, 3 * head_dim)
    queries = layer_norm(projected[..., :head_dim], query_gain).astype(jnp.bfloat16)
    keys_normed = layer_norm(projected[..., head_dim : 2 * head_dim], key_gain).astype(jnp.bfloat16)
    values = projected[..., 2 * head_dim :].astype(jnp.bfloat16)
    scores = jnp.einsum(
        "iphd,iqhd->ihpq", queries, keys_normed, preferred_element_type=jnp.float32
    ) / math.sqrt(head_dim)
    probabilities = jax.nn.softmax(scores, axis=-1).astype(jnp.bfloat16)
    mixed = jnp.einsum("ihpq,iqhd->iphd", probabilities, values, preferred_element_type=jnp.float32)
    mixed = mixed.astype(jnp.bfloat16).reshape(tok_rows, local_heads * head_dim)
    product = lax.dot_general(
        mixed,
        lax.all_gather(project_out, "rep", axis=0, tiled=True),
        (((1,), (1,)), ((), ())),
        preferred_element_type=jnp.float32,
    )
    attended = lax.psum_scatter(product.astype(jnp.bfloat16), "tp", scatter_dimension=1, tiled=True)
    local_in = jnp.sum(jnp.square(project_in.astype(jnp.float32)))
    local_out = jnp.sum(jnp.square(project_out.astype(jnp.float32)))
    total_in, total_out = lax.psum((local_in, local_out), ("rep", "tp"))
    weight_norms = jnp.stack([jnp.sqrt(total_in / (3 * HEADS * HEAD_DIM)), jnp.sqrt(total_out / D)])
    return (attended, weight_norms)


def solution(mesh):
    in_specs = (P("rep", "tp"), P(), P(), P(), P("rep", "tp", None), P("rep", "tp"))
    out_specs = (P("rep", "tp"), P())
    return jax.shard_map(shards, mesh=mesh, in_specs=in_specs, out_specs=out_specs, check_vma=False)
```

profile of v0, /device:TPU:0, one launch (start us, length us, event | category | flops | bytes accessed | tf_op | source)
XLA Modules:
  0.0 571.8 jit_solution(6341764529476445264)
XLA Ops:
  7.2 0.0 all-gather.4.cloned.1.call-start
  7.2 0.7 all-gather.4.cloned.1.call-update
  7.9 0.0 all-gather.6.cloned.1.call-start
  7.9 6.0 %copy.10 = bf16[384,12,384]{0,2,1:T(8,128)(2,1)} copy(bf16[384,12,384]{2,0,1:T(8,128)(2,1)} %param.10) | data formatting | bytes 7077888 | tf_op args[4]
  14.0 0.0 all-gather.6.cloned.1.call-update
  14.0 0.0 all-gather.8.cloned.1.call-start
  14.1 0.0 copy-start.3
  14.1 0.7 all-gather.8.cloned.1.call-update
  14.7 0.0 reduce-scatter.2.cloned.1.call-start
  14.8 77.8 %all-gather.4.cloned.1.call-done = bf16[512,6144]{1,0:T(8,128)(2,1)} async-done(((bf16[512,3072]{1,0:T(8,128)(2,1)}), bf16[512,6144]{1,0:T(8,128)(2,1)}) %all-gather.4.cloned.1.call-update) | async-done | bytes 6291472 | tf_op jit(solution)/shard_map/all_gather | solution.py:21
  92.6 0.0 copy-start
  92.6 3.8 convert_reduce_fusion
  96.5 0.7 copy-done
  97.2 1.8 fusion.5
  99.0 0.0 copy-done.3
  99.0 6.3 %fusion.7 = bf16[512,6144]{1,0:T(8,128)(2,1)} fusion(bf16[512,6144]{1,0:T(8,128)(2,1)S(1)} %copy-done, f32[6144]{0:T(1024)S(1)} %copy-done.3, f32[512]{0:T(512)S(1)} %add_rsqrt_fusion.2, f32[512]{0:T(512)S(1)} %broadcast_multiply_fusion.2), kind=kLoop, calls=%fused_computation.9 | loop fusion | flops 15728640 | bytes 12611584 | tf_op jit(solution)/shard_map/convert_element_type | solution.py:22
  105.3 265.2 %all-gather.6.cloned.1.call-done = bf16[6144,12,384]{0,2,1:T(8,128)(2,1)} async-done(((bf16[384,12,384]{0,2,1:T(8,128)(2,1)}), bf16[6144,12,384]{0,2,1:T(8,128)(2,1)}) %all-gather.6.cloned.1.call-update) | async-done | bytes 56623120 | tf_op jit(solution)/shard_map/all_gather | solution.py:26
  370.5 37.1 %fusion.1 = f32[2,256,12,384]{3,1,2,0:T(8,128)} fusion(bf16[2,256,6144,1]{2,1,3,0:T(8,128)(2,1)} %bitcast.26, bf16[6144,12,384]{0,2,1:T(8,128)(2,1)} %all-gather.6.cloned.1.call-done), kind=kOutput, calls=%fused_computation.1 | convolution fusion | flops 28991029248 | bytes 72351744 | tf_op jit(solution)/shard_map/dot_general | solution.py:27
  407.6 0.0 copy-start.1
  407.6 0.0 copy-start.4
  407.6 0.0 copy-start.5
  407.6 4.7 slice_reduce_fusion.1
  412.4 5.8 %multiply_reduce_fusion.3 = (f32[2,256,12]{1,2,0:T(8,128)S(1)}, f32[2,256,12]{1,2,0:T(8,128)S(1)}) fusion(f32[2,256,12,384]{3,1,2,0:T(8,128)} %fusion.1, f32[2,256,12]{1,2,0:T(8,128)S(1)} %get-tuple-element.11, f32[2,256,12]{1,2,0:T(8,128)S(1)} %get-tuple-element.10), kind=kLoop, calls=%fused_computation.21 | loop fusion | flops 4706304 | bytes 6389760 | tf_op jit(solution)/shard_map/reduce_sum | solution.py:16
  418.3 0.0 copy-done.1
  418.3 0.0 copy-done.4
  418.3 0.0 copy-done.5
  418.3 3.5 fusion.14
  421.8 5.0 fusion.23
  426.8 0.9 fusion.21
  427.7 1.6 copy.13
  429.3 0.3 copy.17
  429.7 41.3 %all-gather.8.cloned.1.call-done = bf16[6144,1536]{1,0:T(8,128)(2,1)} async-done(((bf16[384,1536]{1,0:T(8,128)(2,1)}), bf16[6144,1536]{1,0:T(8,128)(2,1)}) %all-gather.8.cloned.1.call-update) | async-done | bytes 18874384 | tf_op jit(solution)/shard_map/all_gather | solution.py:42
  471.0 15.6 %convolution_convert_fusion = bf16[512,6144]{1,0:T(8,128)(2,1)} fusion(bf16[512,1536]{0,1:T(8,128)(2,1)S(1)} %bitcast.28, bf16[6144,1536]{1,0:T(8,128)(2,1)} %all-gather.8.cloned.1.call-done), kind=kOutput, calls=%fused_computation.10 | convolution fusion | flops 9666822144 | bytes 26738688 | tf_op jit(solution)/shard_map/dot_general | solution.py:40
  486.6 0.0 copy-start.2
  486.6 0.0 reduce-scatter.2.cloned.1.call-update
  486.6 2.0 copy-done.2
  488.6 2.4 multiply_reduce_fusion
  491.0 2.5 multiply_reduce_fusion.4
  493.5 41.4 %all-reduce = (f32[]{:T(128)}, f32[]{:T(128)}) all-reduce(f32[]{:T(128)} %multiply_reduce_fusion.4, f32[]{:T(128)} %multiply_reduce_fusion), channel_id=1, replica_groups=mesh['rep'=16,'tp'=2] {'rep','tp'}, use_global_device_ids=true, to_apply=%region_12.0 | all-reduce | flops 2 | bytes 16 | tf_op jit(solution)/shard_map/psum | solution.py:49
  536.2 0.6 pad_maximum_fusion
  536.8 28.5 %reduce-scatter.2.cloned.1.call-done = bf16[512,3072]{1,0:T(8,128)(2,1)} async-done(((bf16[512,6144]{1,0:T(8,128)(2,1)}), bf16[512,3072]{1,0:T(8,128)(2,1)}) %reduce-scatter.2.cloned.1.call-update) | async-done | bytes 3145744 | tf_op jit(solution)/shard_map/reduce_scatter | solution.py:46
  (5 shorter events, 0.0 us)
Async XLA Ops:
  7.2 85.5 %all-gather.4.cloned.1.call-start = ((), (), s32[]{:S(2)}) async-start(), calls=%async_computation.1 | async-start | bytes 9437184 | tf_op jit(solution)/shard_map/all_gather | solution.py:21
  7.9 362.6 %all-gather.6.cloned.1.call-start = ((), (), s32[]{:S(2)}) async-start(), calls=%async_computation.2 | async-start | bytes 60162048 | tf_op jit(solution)/shard_map/all_gather | solution.py:26
  14.0 457.0 %all-gather.8.cloned.1.call-start = ((), (), s32[]{:S(2)}) async-start(), calls=%async_computation.3 | async-start | bytes 20054016 | tf_op jit(solution)/shard_map/all_gather | solution.py:42
  14.1 85.0 %copy-start.3 = (f32[6144]{0:T(1024)S(1)}, f32[6144]{0:T(1024)}, u32[]{:S(2)}) copy-start(f32[6144]{0:T(1024)} %param.7) | copy-start | bytes 73732
  14.7 550.6 %reduce-scatter.2.cloned.1.call-start = ((), (), s32[]{:S(2)}) async-start(), calls=%async_computation.4 | async-start | bytes 9437184 | tf_op jit(solution)/shard_map/reduce_scatter | solution.py:46
  92.6 4.6 copy-start
  407.6 10.6 %copy-start.1 = (f32[2,256,12,384]{3,1,2,0:T(8,128)S(1)}, f32[2,256,12,384]{3,1,2,0:T(8,128)}, u32[]{:S(2)}) copy-start(f32[2,256,12,384]{3,1,2,0:T(8,128)} %fusion.1) | copy-start | bytes 28311556
  407.6 10.6 %copy-start.4 = (f32[128]{0:T(128)S(1)}, f32[128]{0:T(128)}, u32[]{:S(2)}) copy-start(f32[128]{0:T(128)} %param.9) | copy-start | bytes 1540
  407.6 10.6 %copy-start.5 = (f32[128]{0:T(128)S(1)}, f32[128]{0:T(128)}, u32[]{:S(2)}) copy-start(f32[128]{0:T(128)} %param.8) | copy-start | bytes 1540
  486.6 2.0 copy-start.2
Sparse Core Ops, SparseCore 0:
  9.5 83.0 all-gather.3
  94.2 276.2 all-gather.5
  372.1 98.8 all-gather.7
  486.8 78.5 reduce-scatter.1
where the time goes:
time: 572 us
  waiting for transfers between devices  414 us (72%)
  matrix products  57.2 us (10%)
  blocking collectives  41.4 us (7%)
  other arithmetic  33 us (6%)
  between operations  15.2 us (3%)
  local copies, waits for them, and re-layouts  10.7 us (2%)
    all_gather x1, waiting for transfers between devices, shards(): piece = lax.all_gather(project_in, 'rep', axis=0, tiled=True)  265 us
    all_gather x1, waiting for transfers between devices, shards(): gathered_rows = lax.all_gather(activations, 'tp', axis=1, tiled=True)  77.8 us
    psum x1, blocking collectives, shards(): total_in, total_out = lax.psum((local_in, local_out), ('rep', 'tp'))  41.4 us
    all_gather x1, waiting for transfers between devices, shards(): lax.all_gather(project_out, 'rep', axis=0, tiled=True)  41.3 us
    dot_general x1, matrix products, shards(): jnp.dot(normed, piece.reshape(piece.shape[0], -1), preferred_element_type...  37.1 us
    reduce_scatter x1, waiting for transfers between devices, shards(): lax.psum_scatter(product.astype(jnp.bfloat16), 'tp', scatter_dimension=1,...  28.5 us
    dot_general x1, matrix products, shards(): lax.dot_general(mixed, lax.all_gather(project_out, 'rep', axis=0, tiled=T...  15.6 us
  transfers between devices with their start and end apart: 4, of which 4 were waited for; matrix products, arithmetic and copies ran while one was open for 14% of the time, Pallas kernels for 0%

commit v1 on v0

--- a/solution.py
+++ b/solution.py
@@ -18,7 +18,7 @@
 
 
 def shards(activations, norm_gain, query_gain, key_gain, project_in, project_out):
-    gathered_rows = lax.all_gather(activations, "tp", axis=1, tiled=True)
+    gathered_rows = jnp.concatenate(lax.all_gather(activations, "tp"), axis=1)
     normed = layer_norm(gathered_rows.astype(jnp.float32), norm_gain).astype(jnp.bfloat16)
     tok_rows = normed.shape[0]
     local_heads = project_in.shape[1]

time: 572 us -> 573 us (level)
  waiting for transfers between devices: 414 us -> 361 us
  local copies, waits for them, and re-layouts: 10.7 us -> 54 us
  other arithmetic: 33 us -> 43.3 us
    all_gather x1, waiting for transfers between devices: 265 us -> 211 us  [shards(): piece = lax.all_gather(project_in, 'rep', axis=0, tiled=True)]
    mul x0 -> x2, local copies, waits for them, and re-layouts: none -> 29.5 us  [layer_norm(): return centred * lax.rsqrt(variance + 1e-06) * gain]
    convert_element_type x0 -> x1, local copies, waits for them, and re-layouts: none -> 14.5 us  [shards(): layer_norm(gathered_rows.astype(jnp.float32), norm_gain)]
  transfers between devices with their start and end apart: 4 -> 4, of which waited for: 4 -> 4; matrix products, arithmetic and copies ran while one was open for 14% -> 24% of each run, Pallas kernels for 0% -> 0%
where the time goes in v1:
time: 573 us; the launch traced here: 572 us
  waiting for transfers between devices  361 us (63%)
  matrix products  57.1 us (10%)
  local copies, waits for them, and re-layouts  54 us (9%)
  other arithmetic  43.3 us (8%)
  blocking collectives  41.4 us (7%)
  between operations  15.2 us (3%)
    all_gather x1, waiting for transfers between devices, shards(): piece = lax.all_gather(project_in, 'rep', axis=0, tiled=True)  211 us
    all_gather x1, waiting for transfers between devices, shards(): gathered_rows = jnp.concatenate(lax.all_gather(activations, 'tp'), axis=1)  77.8 us
    all_gather x1, waiting for transfers between devices, shards(): lax.all_gather(project_out, 'rep', axis=0, tiled=True)  41.4 us
    psum x1, blocking collectives, shards(): total_in, total_out = lax.psum((local_in, local_out), ('rep', 'tp'))  41.4 us
    dot_general x1, matrix products, shards(): jnp.dot(normed, piece.reshape(piece.shape[0], -1), preferred_element_type...  37.1 us
    mul x2, local copies, waits for them, and re-layouts, layer_norm(): return centred * lax.rsqrt(variance + 1e-06) * gain  29.5 us
    reduce_scatter x1, waiting for transfers between devices, shards(): lax.psum_scatter(product.astype(jnp.bfloat16), 'tp', scatter_dimension=1,...  28.5 us
    dot_general x1, matrix products, shards(): lax.dot_general(mixed, lax.all_gather(project_out, 'rep', axis=0, tiled=T...  15.6 us
  transfers between devices with their start and end apart: 4, of which 4 were waited for; matrix products, arithmetic and copies ran while one was open for 24% of the time, Pallas kernels for 0%

profile of v1, /device:TPU:0, one launch (start us, length us, event | category | flops | bytes accessed | tf_op | source)
XLA Modules:
  0.0 571.8 jit_solution(8365091709977114880)
XLA Ops:
  7.2 0.0 all-gather.9.cloned.1.call-start
  7.2 0.7 all-gather.9.cloned.1.call-update
  7.9 0.0 copy-start.2
  7.9 0.0 all-gather.5.cloned.1.call-start
  8.0 6.0 %copy.17 = bf16[384,12,384]{0,2,1:T(8,128)(2,1)} copy(bf16[384,12,384]{2,0,1:T(8,128)(2,1)} %param.10) | data formatting | bytes 7077888 | tf_op args[4]
  14.0 0.0 all-gather.5.cloned.1.call-update
  14.0 0.0 all-gather.7.cloned.1.call-start
  14.1 0.7 all-gather.7.cloned.1.call-update
  14.8 0.0 reduce-scatter.2.cloned.1.call-start
  14.8 0.0 copy-done.2
  14.8 77.8 %all-gather.9.cloned.1.call-done = bf16[1024,3072]{1,0:T(8,128)(2,1)} async-done(((bf16[512,3072]{1,0:T(8,128)(2,1)}), bf16[1024,3072]{1,0:T(8,128)(2,1)}) %all-gather.9.cloned.1.call-update) | async-done | bytes 6291472 | tf_op jit(solution)/shard_map/all_gather | solution.py:21
  92.6 0.0 slice-start
  92.6 3.8 convert_reduce_fusion
  96.5 0.0 slice-start.1
  96.5 9.9 %convert_element_type.56 = f32[1024,3072]{1,0:T(8,128)} convert(bf16[1024,3072]{1,0:T(8,128)(2,1)} %all-gather.9.cloned.1.call-done) | non-fusion elementwise | flops 3145728 | bytes 18874368 | tf_op jit(solution)/shard_map/convert_element_type | solution.py:22
  106.4 5.9 %multiply_reduce_fusion = f32[512]{0:T(512)S(1)} fusion(f32[2,512,3072]{2,1,0:T(8,128)} %bitcast.29, f32[512]{0:T(512)S(1)} %broadcast_multiply_fusion.2), kind=kLoop, calls=%fused_computation.4 | loop fusion | flops 9436672 | bytes 12587008 | tf_op jit(solution)/shard_map/reduce_sum | solution.py:16
  112.3 0.0 slice-done
  112.3 0.0 slice-done.1
  112.4 2.6 fusion.3
  115.0 29.5 %copy.16 = bf16[512,2,3072]{2,1,0:T(2,128)(2,1)} copy(bf16[512,2,3072]{2,0,1:T(8,128)(2,1)S(1)} %fusion.3) | data formatting | bytes 12582912 | tf_op jit(solution)/shard_map/mul | solution.py:17
  144.5 14.5 %reshape.100 = bf16[2,256,6144,1]{2,1,0,3:T(8,128)(2,1)} reshape(bf16[512,2,3072]{2,1,0:T(2,128)(2,1)} %copy.16) | data formatting | bytes 12582912 | tf_op jit(solution)/shard_map/convert_element_type | solution.py:22
  159.0 211.5 %all-gather.5.cloned.1.call-done = bf16[6144,12,384]{0,2,1:T(8,128)(2,1)} async-done(((bf16[384,12,384]{0,2,1:T(8,128)(2,1)}), bf16[6144,12,384]{0,2,1:T(8,128)(2,1)}) %all-gather.5.cloned.1.call-update) | async-done | bytes 56623120 | tf_op jit(solution)/shard_map/all_gather | solution.py:26
  370.5 37.1 %fusion.1 = f32[2,256,12,384]{3,1,2,0:T(8,128)} fusion(bf16[6144,12,384]{0,2,1:T(8,128)(2,1)} %all-gather.5.cloned.1.call-done, bf16[2,256,6144,1]{2,1,0,3:T(8,128)(2,1)} %reshape.100), kind=kOutput, calls=%fused_computation.1 | convolution fusion | flops 28991029248 | bytes 72351744 | tf_op jit(solution)/shard_map/dot_general | solution.py:27
  407.6 0.0 copy-start
  407.6 0.0 copy-start.3
  407.6 0.0 copy-start.4
  407.6 4.7 slice_reduce_fusion.1
  412.4 6.0 %multiply_reduce_fusion.4 = (f32[2,256,12]{1,2,0:T(8,128)S(1)}, f32[2,256,12]{1,2,0:T(8,128)S(1)}) fusion(f32[2,256,12,384]{3,1,2,0:T(8,128)} %fusion.1, f32[2,256,12]{1,2,0:T(8,128)S(1)} %get-tuple-element.11, f32[2,256,12]{1,2,0:T(8,128)S(1)} %get-tuple-element.10), kind=kLoop, calls=%fused_computation.19 | loop fusion | flops 4706304 | bytes 6389760 | tf_op jit(solution)/shard_map/reduce_sum | solution.py:16
  418.4 0.0 copy-done
  418.4 0.0 copy-done.3
  418.4 0.0 copy-done.4
  418.4 3.5 fusion.11
  422.0 4.8 fusion.20
  426.8 0.9 fusion.18
  427.6 1.6 copy.20
  429.3 0.3 copy.24
  429.6 41.4 %all-gather.7.cloned.1.call-done = bf16[6144,1536]{1,0:T(8,128)(2,1)} async-done(((bf16[384,1536]{1,0:T(8,128)(2,1)}), bf16[6144,1536]{1,0:T(8,128)(2,1)}) %all-gather.7.cloned.1.call-update) | async-done | bytes 18874384 | tf_op jit(solution)/shard_map/all_gather | solution.py:42
  471.0 15.6 %convolution_convert_fusion = bf16[512,6144]{1,0:T(8,128)(2,1)} fusion(bf16[512,1536]{0,1:T(8,128)(2,1)S(1)} %bitcast.31, bf16[6144,1536]{1,0:T(8,128)(2,1)} %all-gather.7.cloned.1.call-done), kind=kOutput, calls=%fused_computation.5 | convolution fusion | flops 9666822144 | bytes 26738688 | tf_op jit(solution)/shard_map/dot_general | solution.py:40
  486.6 0.0 copy-start.1
  486.6 0.0 reduce-scatter.2.cloned.1.call-update
  486.6 2.0 copy-done.1
  488.6 2.4 multiply_reduce_fusion.1
  491.0 2.5 multiply_reduce_fusion.5
  493.5 41.4 %all-reduce = (f32[]{:T(128)}, f32[]{:T(128)}) all-reduce(f32[]{:T(128)} %multiply_reduce_fusion.5, f32[]{:T(128)} %multiply_reduce_fusion.1), channel_id=1, replica_groups=mesh['rep'=16,'tp'=2] {'rep','tp'}, use_global_device_ids=true, to_apply=%region_12.0 | all-reduce | flops 2 | bytes 16 | tf_op jit(solution)/shard_map/psum | solution.py:49
  536.2 0.6 pad_maximum_fusion
  536.8 28.5 %reduce-scatter.2.cloned.1.call-done = bf16[512,3072]{1,0:T(8,128)(2,1)} async-done(((bf16[512,6144]{1,0:T(8,128)(2,1)}), bf16[512,3072]{1,0:T(8,128)(2,1)}) %reduce-scatter.2.cloned.1.call-update) | async-done | bytes 3145744 | tf_op jit(solution)/shard_map/reduce_scatter | solution.py:46
  (9 shorter events, 0.1 us)
Async XLA Ops:
  7.2 85.5 %all-gather.9.cloned.1.call-start = ((), (), s32[]{:S(2)}) async-start(), calls=%async_computation.4 | async-start | bytes 9437184 | tf_op jit(solution)/shard_map/all_gather | solution.py:21
  7.9 6.9 %copy-start.2 = (f32[6144]{0:T(1024)S(1)}, f32[6144]{0:T(1024)}, u32[]{:S(2)}) copy-start(f32[6144]{0:T(1024)} %param.7) | copy-start | bytes 73732
  7.9 362.6 %all-gather.5.cloned.1.call-start = ((), (), s32[]{:S(2)}) async-start(), calls=%async_computation.1 | async-start | bytes 60162048 | tf_op jit(solution)/shard_map/all_gather | solution.py:26
  14.0 457.0 %all-gather.7.cloned.1.call-start = ((), (), s32[]{:S(2)}) async-start(), calls=%async_computation.2 | async-start | bytes 20054016 | tf_op jit(solution)/shard_map/all_gather | solution.py:42
  14.8 550.5 %reduce-scatter.2.cloned.1.call-start = ((), (), s32[]{:S(2)}) async-start(), calls=%async_computation.3 | async-start | bytes 9437184 | tf_op jit(solution)/shard_map/reduce_scatter | solution.py:46
  92.6 19.7 %slice-start = ((s8[6291456]{0:T(1024)(128)(4,1)}), s8[2097152]{0:T(1024)(128)(4,1)S(1)}, s32[]{:S(2)}) async-start(s8[6291456]{0:T(1024)(128)(4,1)} %bitcast.27), calls=%async_computation.5 | async-start | bytes 4194304
  96.5 15.9 %slice-start.1 = ((s8[6291456]{0:T(1024)(128)(4,1)}), s8[4194304]{0:T(1024)(128)(4,1)S(1)}, s32[]{:S(2)}) async-start(s8[6291456]{0:T(1024)(128)(4,1)} %bitcast.27), calls=%async_computation.6 | async-start | bytes 8388608
  407.6 10.8 %copy-start = (f32[2,256,12,384]{3,1,2,0:T(8,128)S(1)}, f32[2,256,12,384]{3,1,2,0:T(8,128)}, u32[]{:S(2)}) copy-start(f32[2,256,12,384]{3,1,2,0:T(8,128)} %fusion.1) | copy-start | bytes 28311556
  407.6 10.8 %copy-start.3 = (f32[128]{0:T(128)S(1)}, f32[128]{0:T(128)}, u32[]{:S(2)}) copy-start(f32[128]{0:T(128)} %param.9) | copy-start | bytes 1540
  407.6 10.8 %copy-start.4 = (f32[128]{0:T(128)S(1)}, f32[128]{0:T(128)}, u32[]{:S(2)}) copy-start(f32[128]{0:T(128)} %param.8) | copy-start | bytes 1540
  486.6 2.0 copy-start.1
Sparse Core Ops, SparseCore 0:
  9.5 83.0 all-gather.8
  94.2 276.2 all-gather.4
  372.1 98.8 all-gather.6
  486.8 78.5 reduce-scatter.1
